TPU v7x, 32 devices: a whole 2x2x4 slice. The times are simulated.
32 devices in a mesh: dp: 2 (over x), mp: 16 (over z, y, core).
Axes of the slice: x: 2, y: 2, z: 4, core: 2. Of those that a mesh axis runs over, the one named last changes fastest.
Arguments:
- base_rows: bfloat16 [256, 8192], P('dp', 'mp'), may hold values from -6 to 6
- layer_rows: bfloat16 [256, 8192], P('dp', 'mp'), may hold values from -6 to 6
- cross_weight: bfloat16 [8192, 8192], P(None, 'mp'), may hold values from -0.0625 to 0.0625
- cross_bias: float32 [8192], P('mp'), may hold values from -3 to 3
- upstream: bfloat16 [256, 8192], P('dp', 'mp'), may hold values from -6 to 6
Outputs:
- crossed: bfloat16 [256, 8192], P('dp', 'mp')
- grad_base: bfloat16 [256, 8192], P('dp', 'mp')
- grad_layer: bfloat16 [256, 8192], P('dp', 'mp')
- grad_weight: float32 [8192, 8192], P('dp', 'mp')
- grad_bias: float32 [8192], P('mp')
All inputs are finite; a program needn't handle non-finite values.
Results may differ from a plain program's by a relative error of at most 0.0041.
Values may be sent and summed in bfloat16 or wider, within the bound.
No kernel may reach another device: no remote copies, remote signals or barrier semaphores. Data moves between devices by JAX's collectives and lax.ppermute only.
A program may use at most 128 MiB of HBM per device.

v0:
```python
import jax
import jax.numpy as jnp
from jax import lax
from jax.sharding import PartitionSpec as P


def local(base_rows, layer_rows, cross_weight, cross_bias, upstream):
    groups = lax.axis_size("dp")
    row_block = lax.all_to_all(cross_weight, "mp", split_axis=0, concat_axis=1, tiled=True)
    full_rows = lax.all_gather(layer_rows, "mp", axis=1, tiled=True)
    mixed = jnp.dot(full_rows, cross_weight, preferred_element_type=jnp.float32) + cross_bias
    base = base_rows.astype(jnp.float32)
    crossed = (base * mixed + layer_rows.astype(jnp.float32)).astype(jnp.bfloat16)
    upper = upstream.astype(jnp.float32)
    delta = upper * base
    delta_low = delta.astype(jnp.bfloat16)
    grad_base = (upper * mixed).astype(jnp.bfloat16)
    back = lax.dot_general(
        lax.all_gather(delta_low, "mp", axis=1, tiled=True),
        row_block,
        (((1,), (1,)), ((), ())),
        preferred_element_type=jnp.float32,
    )
    grad_layer = (upper + back).astype(jnp.bfloat16)
    scale = jnp.float32(base_rows.shape[0] * groups) ** (-0.5)
    grad_weight = (
        lax.psum_scatter(
            lax.dot_general(
                full_rows, delta_low, (((0,), (0,)), ((), ())), preferred_element_type=jnp.float32
            ),
            "dp",
            scatter_dimension=0,
            tiled=True,
        )
        * scale
    )
    grad_bias = lax.psum(jnp.sum(delta, axis=0), "dp") * scale
    return (crossed, grad_base, grad_layer, grad_weight, grad_bias)


def solution(mesh):
    return jax.shard_map(
        local,
        mesh=mesh,
        in_specs=(P("dp", "mp"), P("dp", "mp"), P(None, "mp"), P("mp"), P("dp", "mp")),
        out_specs=(P("dp", "mp"), P("dp", "mp"), P("dp", "mp"), P("dp", "mp"), P("mp")),
        check_vma=False,
    )
```

profile of v0, /device:TPU:0, one launch (start us, length us, event | category | flops | bytes accessed | tf_op | source)
XLA Modules:
  0.0 428.7 jit_solution(16000133492980373238)
XLA Ops:
  7.2 0.0 all-gather.3.cloned.1.call-start
  7.2 0.7 all-gather.3.cloned.1.call-update
  7.9 0.0 all-gather.5.cloned.1.call-start
  7.9 46.0 %all-gather.3.cloned.1.call-done = bf16[128,8192]{1,0:T(8,128)(2,1)} async-done(((bf16[128,512]{1,0:T(8,128)(2,1)}), bf16[128,8192]{1,0:T(8,128)(2,1)}) %all-gather.3.cloned.1.call-update) | async-done | bytes 2097168 | tf_op jit(solution)/shard_map/all_gather | solution.py:10
  53.9 0.0 copy-start
  53.9 6.2 %fusion.3 = (bf16[128,512]{1,0:T(8,128)(2,1)}, bf16[128,512]{1,0:T(8,128)(2,1)}, bf16[128,512]{1,0:T(8,128)(2,1)}, f32[512]{0:T(512)S(1)}) fusion(bf16[128,512]{1,0:T(8,128)(2,1)} %param.9, bf16[128,512]{1,0:T(8,128)(2,1)} %param.6, bf16[128,512]{1,0:T(8,128)(2,1)} %param.5, f32[512]{0:T(512)} %param.8, bf16[128,8192]{1,0:T(8,128)(2,1)} %all-gather.3.cloned.1.call-done, ...), kind=kOutput, calls=%fused_computation.10 | convolution fusion | flops 1074527744 | bytes 11276288 | tf_op jit(solution)/shard_map/dot_general | solution.py:11
  60.1 0.0 all-gather.5.cloned.1.call-update
  60.2 0.0 reduce-scatter.2.cloned.1.call-start
  60.2 0.0 copy-done
  60.2 9.0 %convolution_bitcast_fusion = f32[8192,512]{0,1:T(8,128)} fusion(bf16[128,512]{1,0:T(8,128)(2,1)} %get-tuple-element.24, bf16[128,8192]{1,0:T(8,128)(2,1)S(1)} %copy-done), kind=kOutput, calls=%fused_computation | convolution fusion | flops 1073741824 | bytes 19005440 | tf_op jit(solution)/shard_map/dot_general | solution.py:28
  69.2 0.0 reduce-scatter.2.cloned.1.call-update
  69.2 4.8 %all-to-all-start = ((bf16[16,512,512]{2,1,0:T(8,128)(2,1)}), bf16[16,512,512]{2,1,0:T(8,128)(2,1)}, u32[]{:S(2)}, u32[]{:S(2)}) async-start(bf16[16,512,512]{2,1,0:T(8,128)(2,1)} %bitcast.12), calls=%async_computation | async-start | bytes 16777216 | tf_op jit(solution)/shard_map/all_to_all | solution.py:9
  74.0 4.9 %psum.7 = f32[512]{0:T(512)S(1)} all-reduce(f32[512]{0:T(512)S(1)} %get-tuple-element.25), channel_id=1, replica_groups=mesh['dp'=2,'mp'=16] {'dp'}, use_global_device_ids=true, to_apply=%region_2.0 | all-reduce | flops 512 | bytes 4096 | tf_op jit(solution)/shard_map/psum | solution.py:37
  79.0 0.6 broadcast_multiply_fusion.1
  79.6 154.0 %all-to-all-done = bf16[16,512,512]{2,1,0:T(8,128)(2,1)} async-done(((bf16[16,512,512]{2,1,0:T(8,128)(2,1)}), bf16[16,512,512]{2,1,0:T(8,128)(2,1)}, u32[]{:S(2)}, u32[]{:S(2)}) %all-to-all-start) | async-done | bytes 8388640 | tf_op jit(solution)/shard_map/all_to_all | solution.py:9
  233.6 0.0 copy-start.1
  233.6 12.3 %copy.12 = bf16[512,16,512]{0,2,1:T(8,128)(2,1)} copy(bf16[512,16,512]{2,0,1:T(8,128)(2,1)} %bitcast.1) | data formatting | bytes 16777216 | tf_op jit(solution)/shard_map/all_to_all | solution.py:9
  245.9 0.0 all-gather.5.cloned.1.call-done
  245.9 0.0 copy-done.1
  245.9 6.2 %fusion = bf16[128,512]{1,0:T(8,128)(2,1)} fusion(bf16[128,8192]{1,0:T(8,128)(2,1)} %all-gather.5.cloned.1.call-done, bf16[512,8192]{0,1:T(8,128)(2,1)} %bitcast.11, bf16[128,512]{1,0:T(8,128)(2,1)S(1)} %copy-done.1), kind=kOutput, calls=%fused_computation.4 | convolution fusion | flops 1073938432 | bytes 10747904 | tf_op jit(solution)/shard_map/dot_general | solution.py:18
  252.1 153.4 %reduce-scatter.2.cloned.1.call-done = f32[4096,512]{0,1:T(8,128)} async-done(((f32[8192,512]{0,1:T(8,128)}), f32[4096,512]{0,1:T(8,128)}) %reduce-scatter.2.cloned.1.call-update) | async-done | bytes 8388624 | tf_op jit(solution)/shard_map/reduce_scatter | solution.py:27
  405.5 7.8 %broadcast_multiply_fusion = f32[4096,512]{0,1:T(8,128)} fusion(f32[4096,512]{0,1:T(8,128)} %reduce-scatter.2.cloned.1.call-done), kind=kLoop, calls=%fused_computation.1 | loop fusion | flops 2097152 | bytes 16777216 | tf_op jit(solution)/shard_map/mul | solution.py:27
  413.3 8.9 %copy.13 = f32[4096,512]{1,0:T(8,128)} copy(f32[4096,512]{0,1:T(8,128)} %broadcast_multiply_fusion) | data formatting | bytes 16777216
Async XLA Ops:
  7.2 46.8 %all-gather.3.cloned.1.call-start = ((), (), s32[]{:S(2)}) async-start(), calls=%async_computation.2 | async-start | bytes 2228224 | tf_op jit(solution)/shard_map/all_gather | solution.py:10
  7.9 238.0 %all-gather.5.cloned.1.call-start = ((), (), s32[]{:S(2)}) async-start(), calls=%async_computation.3 | async-start | bytes 2228224 | tf_op jit(solution)/shard_map/all_gather | solution.py:19
  53.9 6.3 %copy-start = (bf16[128,8192]{1,0:T(8,128)(2,1)S(1)}, bf16[128,8192]{1,0:T(8,128)(2,1)}, u32[]{:S(2)}) copy-start(bf16[128,8192]{1,0:T(8,128)(2,1)} %all-gather.3.cloned.1.call-done) | copy-start | bytes 6291460
  60.2 345.3 %reduce-scatter.2.cloned.1.call-start = ((), (), s32[]{:S(2)}) async-start(), calls=%async_computation.4 | async-start | bytes 25165824 | tf_op jit(solution)/shard_map/reduce_scatter | solution.py:27
  69.2 164.3 %all-to-all-start = ((bf16[16,512,512]{2,1,0:T(8,128)(2,1)}), bf16[16,512,512]{2,1,0:T(8,128)(2,1)}, u32[]{:S(2)}, u32[]{:S(2)}) async-start(bf16[16,512,512]{2,1,0:T(8,128)(2,1)} %bitcast.12), calls=%async_computation | async-start | bytes 16777216 | tf_op jit(solution)/shard_map/all_to_all | solution.py:9
  233.6 12.3 %copy-start.1 = (bf16[128,512]{1,0:T(8,128)(2,1)S(1)}, bf16[128,512]{1,0:T(8,128)(2,1)}, u32[]{:S(2)}) copy-start(bf16[128,512]{1,0:T(8,128)(2,1)} %param.9) | copy-start | bytes 393220
Sparse Core Ops, SparseCore 0:
  10.1 43.7 all-gather.2
  60.3 143.4 all-gather.4
  206.1 199.3 reduce-scatter.1
where the time goes:
time: 429 us
  waiting for transfers between devices  354 us (83%)
  matrix products  21.4 us (5%)
  local copies, waits for them, and re-layouts  21.3 us (5%)
  between operations  13.8 us (3%)
  other arithmetic  8.35 us (2%)
  blocking collectives  4.93 us (1%)
  starting transfers between devices  4.92 us (1%)
    all_to_all x1, waiting for transfers between devices, local(): lax.all_to_all(cross_weight, 'mp', split_axis=0, concat_axis=1, tiled=True)  154 us
    reduce_scatter x1, waiting for transfers between devices, local(): lax.psum_scatter(lax.dot_general(full_rows, delta_low, (((0,), (0,)), (()...  153 us
    all_gather x1, waiting for transfers between devices, local(): full_rows = lax.all_gather(layer_rows, 'mp', axis=1, tiled=True)  46 us
    all_to_all x1, local copies, waits for them, and re-layouts, local(): lax.all_to_all(cross_weight, 'mp', split_axis=0, concat_axis=1, tiled=True)  12.3 us
    dot_general x1, matrix products, local(): lax.dot_general(full_rows, delta_low, (((0,), (0,)), ((), ())), preferred...  8.99 us
    unnamed x5, local copies, waits for them, and re-layouts  8.95 us
  transfers between devices with their start and end apart: 4, of which 3 were waited for; matrix products, arithmetic and copies ran while one was open for 7% of the time, Pallas kernels for 0%

commit v1 on v0

--- a/solution.py
+++ b/solution.py
@@ -6,7 +6,9 @@
 
 def local(base_rows, layer_rows, cross_weight, cross_bias, upstream):
     groups = lax.axis_size("dp")
-    row_block = lax.all_to_all(cross_weight, "mp", split_axis=0, concat_axis=1, tiled=True)
+    pieces = jnp.split(cross_weight, lax.axis_size("mp"), axis=0)
+    received = lax.all_to_all(jnp.stack(pieces), "mp", 0, 0)
+    row_block = jnp.concatenate(received, axis=1)
     full_rows = lax.all_gather(layer_rows, "mp", axis=1, tiled=True)
     mixed = jnp.dot(full_rows, cross_weight, preferred_element_type=jnp.float32) + cross_bias
     base = base_rows.astype(jnp.float32)

time: 429 us -> 336 us (0.78)
  the two profiles are of different devices: /device:TPU:0 before, /device:TPU:15 now
where the time goes in v1:
time: 336 us; the launch traced here: 335 us
  waiting for transfers between devices  223 us (66%)
  local copies, waits for them, and re-layouts  59.1 us (18%)
  matrix products  21.2 us (6%)
  between operations  13.8 us (4%)
  other arithmetic  8.35 us (2%)
  starting transfers between devices  5.69 us (2%)
  blocking collectives  4.38 us (1%)
    all_to_all x1, waiting for transfers between devices, local(): received = lax.all_to_all(jnp.stack(pieces), 'mp', 0, 0)  177 us
    unnamed x42, local copies, waits for them, and re-layouts  52.5 us
    all_gather x1, waiting for transfers between devices, local(): full_rows = lax.all_gather(layer_rows, 'mp', axis=1, tiled=True)  44.5 us
    dot_general x1, matrix products, local(): lax.dot_general(full_rows, delta_low, (((0,), (0,)), ((), ())), preferred...  9 us
    mul x1, other arithmetic, local(): lax.psum_scatter(lax.dot_general(full_rows, delta_low, (((0,), (0,)), (()...  7.76 us
  transfers between devices with their start and end apart: 4, of which 2 were waited for; matrix products, arithmetic and copies ran while one was open for 20% of the time, Pallas kernels for 0%

profile of v1, /device:TPU:15, one launch (start us, length us, event | category | flops | bytes accessed | tf_op | source)
XLA Modules:
  0.0 335.1 jit_solution(14075404648504498726)
XLA Ops:
  7.2 0.0 all-gather.3.cloned.1.call-start
  7.2 0.7 all-gather.3.cloned.1.call-update
  7.9 0.0 all-gather.5.cloned.1.call-start
  7.9 44.5 %all-gather.3.cloned.1.call-done = bf16[128,8192]{1,0:T(8,128)(2,1)} async-done(((bf16[128,512]{1,0:T(8,128)(2,1)}), bf16[128,8192]{1,0:T(8,128)(2,1)}) %all-gather.3.cloned.1.call-update) | async-done | bytes 2097168 | tf_op jit(solution)/shard_map/all_gather | solution.py:12
  52.4 0.0 copy-start
  52.4 6.2 %fusion.3 = (bf16[128,512]{1,0:T(8,128)(2,1)}, bf16[128,512]{1,0:T(8,128)(2,1)}, bf16[128,512]{1,0:T(8,128)(2,1)}, f32[512]{0:T(512)S(1)}) fusion(bf16[128,512]{1,0:T(8,128)(2,1)} %param.9, bf16[128,512]{1,0:T(8,128)(2,1)} %param.6, bf16[128,512]{1,0:T(8,128)(2,1)} %param.5, f32[512]{0:T(512)} %param.8, bf16[128,8192]{1,0:T(8,128)(2,1)} %all-gather.3.cloned.1.call-done, ...), kind=kOutput, calls=%fused_computation.26 | convolution fusion | flops 1074527744 | bytes 11276288 | tf_op jit(solution)/shard_map/dot_general | solution.py:13
  58.7 0.0 all-gather.5.cloned.1.call-update
  58.7 0.0 reduce-scatter.2.cloned.1.call-start
  58.7 0.0 copy-done
  58.7 9.0 %convolution_bitcast_fusion = f32[8192,512]{0,1:T(8,128)} fusion(bf16[128,512]{1,0:T(8,128)(2,1)} %get-tuple-element.35, bf16[128,8192]{1,0:T(8,128)(2,1)S(1)} %copy-done), kind=kOutput, calls=%fused_computation | convolution fusion | flops 1073741824 | bytes 19005440 | tf_op jit(solution)/shard_map/dot_general | solution.py:30
  67.7 0.0 reduce-scatter.2.cloned.1.call-update
  67.8 5.7 %fusion.6 = (bf16[512,512]{1,0:T(8,128)(2,1)S(1)}, bf16[512,512]{1,0:T(8,128)(2,1)S(1)}, bf16[512,512]{1,0:T(8,128)(2,1)S(1)}, bf16[512,512]{1,0:T(8,128)(2,1)S(...) fusion(bf16[8192,512]{1,0:T(8,128)(2,1)} %param.7), kind=kLoop, calls=%fused_computation.30 | loop fusion | bytes 16777216 | tf_op jit(solution)/shard_map/split | solution.py:9
  73.5 2.1 copy.28
  75.6 2.1 copy.29
  77.7 2.0 copy.30
  79.7 2.0 copy.31
  81.8 2.1 copy.32
  83.8 2.1 copy.33
  85.9 2.1 copy.34
  88.0 2.0 copy.35
  90.0 2.1 copy.36
  92.1 2.1 copy.37
  94.1 1.0 copy.38
  95.1 0.2 copy.39
  95.3 0.2 copy.40
  95.6 0.2 copy.41
  95.8 0.2 copy.42
  96.0 0.2 copy.43
  96.2 0.0 copy-start.3
  96.2 0.0 copy-start.2
  96.2 0.0 copy-start.1
  96.2 2.0 bitcast_dynamic-update-slice_fusion.15
  98.2 1.9 bitcast_dynamic-update-slice_fusion.14
  100.1 1.9 bitcast_dynamic-update-slice_fusion.13
  102.0 1.9 bitcast_dynamic-update-slice_fusion.12
  103.8 1.9 bitcast_dynamic-update-slice_fusion.11
  105.7 1.9 bitcast_dynamic-update-slice_fusion.10
  107.6 1.9 bitcast_dynamic-update-slice_fusion.9
  109.5 1.9 bitcast_dynamic-update-slice_fusion.8
  111.3 0.0 copy-done.3
  111.3 0.8 bitcast_dynamic-update-slice_fusion.7
  112.2 0.0 copy-done.2
  112.2 0.8 bitcast_dynamic-update-slice_fusion.6
  113.0 0.0 copy-done.1
  113.0 0.8 bitcast_dynamic-update-slice_fusion.5
  113.8 0.8 bitcast_dynamic-update-slice_fusion.4
  114.7 0.8 bitcast_dynamic-update-slice_fusion.3
  115.5 0.8 bitcast_dynamic-update-slice_fusion.2
  116.3 0.8 bitcast_dynamic-update-slice_fusion.1
  117.1 0.8 bitcast_dynamic-update-slice_fusion
  118.0 0.0 copy-start.4
  118.0 5.6 %all-to-all-start = ((bf16[16,512,512]{1,2,0:T(8,128)(2,1)}), bf16[16,512,512]{1,2,0:T(8,128)(2,1)}, u32[]{:S(2)}, u32[]{:S(2)}) async-start(bf16[16,512,512]{1,2,0:T(8,128)(2,1)} %bitcast_dynamic-update-slice_fusion), calls=%async_computation | async-start | bytes 16777216 | tf_op jit(solution)/shard_map/all_to_all | solution.py:10
  123.5 4.4 %psum.7 = f32[512]{0:T(512)S(1)} all-reduce(f32[512]{0:T(512)S(1)} %get-tuple-element.36), channel_id=1, replica_groups=mesh['dp'=2,'mp'=16] {'dp'}, use_global_device_ids=true, to_apply=%region_2.0 | all-reduce | flops 512 | bytes 4096 | tf_op jit(solution)/shard_map/psum | solution.py:39
  127.9 0.6 broadcast_multiply_fusion.1
  128.5 0.0 all-gather.5.cloned.1.call-done
  128.5 177.4 %all-to-all-done = bf16[16,512,512]{1,2,0:T(8,128)(2,1)} async-done(((bf16[16,512,512]{1,2,0:T(8,128)(2,1)}), bf16[16,512,512]{1,2,0:T(8,128)(2,1)}, u32[]{:S(2)}, u32[]{:S(2)}) %all-to-all-start) | async-done | bytes 8388640 | tf_op jit(solution)/shard_map/all_to_all | solution.py:10
  305.9 0.0 copy-done.4
  305.9 5.9 %fusion = bf16[128,512]{1,0:T(8,128)(2,1)} fusion(bf16[128,8192]{1,0:T(8,128)(2,1)} %all-gather.5.cloned.1.call-done, bf16[512,8192]{0,1:T(8,128)(2,1)} %bitcast.17, bf16[128,512]{1,0:T(8,128)(2,1)S(1)} %copy-done.4), kind=kOutput, calls=%fused_computation.4 | convolution fusion | flops 1073938432 | bytes 10747904 | tf_op jit(solution)/shard_map/dot_general | solution.py:20
  311.8 0.0 reduce-scatter.2.cloned.1.call-done
  311.9 7.8 %broadcast_multiply_fusion = f32[4096,512]{0,1:T(8,128)} fusion(f32[4096,512]{0,1:T(8,128)} %reduce-scatter.2.cloned.1.call-done), kind=kLoop, calls=%fused_computation.1 | loop fusion | flops 2097152 | bytes 16777216 | tf_op jit(solution)/shard_map/mul | solution.py:29
  319.6 8.9 %copy.27 = f32[4096,512]{1,0:T(8,128)} copy(f32[4096,512]{0,1:T(8,128)} %broadcast_multiply_fusion) | data formatting | bytes 16777216
Async XLA Ops:
  7.2 45.3 %all-gather.3.cloned.1.call-start = ((), (), s32[]{:S(2)}) async-start(), calls=%async_computation.2 | async-start | bytes 2228224 | tf_op jit(solution)/shard_map/all_gather | solution.py:12
  7.9 120.6 %all-gather.5.cloned.1.call-start = ((), (), s32[]{:S(2)}) async-start(), calls=%async_computation.3 | async-start | bytes 2228224 | tf_op jit(solution)/shard_map/all_gather | solution.py:21
  52.4 6.3 %copy-start = (bf16[128,8192]{1,0:T(8,128)(2,1)S(1)}, bf16[128,8192]{1,0:T(8,128)(2,1)}, u32[]{:S(2)}) copy-start(bf16[128,8192]{1,0:T(8,128)(2,1)} %all-gather.3.cloned.1.call-done) | copy-start | bytes 6291460
  58.7 253.2 %reduce-scatter.2.cloned.1.call-start = ((), (), s32[]{:S(2)}) async-start(), calls=%async_computation.4 | async-start | bytes 25165824 | tf_op jit(solution)/shard_map/reduce_scatter | solution.py:29
  96.2 15.1 %copy-start.3 = (bf16[512,512]{0,1:T(8,128)(2,1)S(1)}, bf16[512,512]{0,1:T(8,128)(2,1)}, u32[]{:S(2)}) copy-start(bf16[512,512]{0,1:T(8,128)(2,1)} %copy.36) | copy-start | bytes 1572868
  96.2 15.9 %copy-start.2 = (bf16[512,512]{0,1:T(8,128)(2,1)S(1)}, bf16[512,512]{0,1:T(8,128)(2,1)}, u32[]{:S(2)}) copy-start(bf16[512,512]{0,1:T(8,128)(2,1)} %copy.37) | copy-start | bytes 1572868
  96.2 16.8 %copy-start.1 = (bf16[512,512]{0,1:T(8,128)(2,1)S(1)}, bf16[512,512]{0,1:T(8,128)(2,1)}, u32[]{:S(2)}) copy-start(bf16[512,512]{0,1:T(8,128)(2,1)} %copy.38) | copy-start | bytes 1572868
  118.0 187.9 %copy-start.4 = (bf16[128,512]{1,0:T(8,128)(2,1)S(1)}, bf16[128,512]{1,0:T(8,128)(2,1)}, u32[]{:S(2)}) copy-start(bf16[128,512]{1,0:T(8,128)(2,1)} %param.9) | copy-start | bytes 393220
  118.0 187.9 %all-to-all-start = ((bf16[16,512,512]{1,2,0:T(8,128)(2,1)}), bf16[16,512,512]{1,2,0:T(8,128)(2,1)}, u32[]{:S(2)}, u32[]{:S(2)}) async-start(bf16[16,512,512]{1,2,0:T(8,128)(2,1)} %bitcast_dynamic-update-slice_fusion), calls=%async_computation | async-start | bytes 16777216 | tf_op jit(solution)/shard_map/all_to_all | solution.py:10
Sparse Core Ops, SparseCore 0:
  10.1 42.2 all-gather.2
  58.8 40.1 all-gather.4
  101.3 187.1 reduce-scatter.1
